TPU v7x, 32 devices: a whole 2x2x4 slice. The times are simulated.
32 devices in a mesh: section: 2 (over x), tensor: 4 (over z), dp: 4 (over y, core).
Axes of the slice: x: 2, y: 2, z: 4, core: 2. Of those that a mesh axis runs over, the one named last changes fastest.
Arguments:
- tokens: bfloat16 [16, 4096], P(None, ('section', 'dp')), may hold values from -100 to 100
- attn_gain: float32 [4096], P(('section', 'dp')), may hold values from 0.1 to 1.9
- qkv_weight: bfloat16 [4096, 10240], P(('section', 'dp'), 'tensor'), may hold values from -0.09375 to 0.09375
- qkv_order: int32 [10], replicated, may hold values from 0 to 9, each once
- cache_keys: bfloat16 [16, 8, 4096, 128], P(('section', 'dp'), 'tensor'), may hold values from -1300 to 1300
- cache_values: bfloat16 [16, 8, 4096, 128], P(('section', 'dp'), 'tensor'), may hold values from -6 to 6
- cache_len: int32 [16], P(('section', 'dp')), may hold values from 2 to 4096, as said below
- out_weight: bfloat16 [8192, 4096], P('tensor', ('section', 'dp')), may hold values from -0.0625 to 0.0625
- ffn_gain: float32 [4096], P(('section', 'dp')), may hold values from 0.1 to 1.9
- gate_up: bfloat16 [2, 4096, 28672], P(None, ('section', 'dp'), 'tensor'), may hold values from -0.09375 to 0.09375
- down_weight: bfloat16 [28672, 4096], P('tensor', ('section', 'dp')), may hold values from -0.03125 to 0.03125
Outputs:
- layer_out: bfloat16 [16, 4096], P(None, ('section', 'dp'))
Inputs may be any that keep to these rules, and one draw needn't show every extreme that they name: qkv_order is a permutation of 0 to 9, the same for every key-value group. `cache_len`: at least one sequence has all 4096 positions valid.
All inputs are finite; a program needn't handle non-finite values.
Results may differ from a plain program's by a relative error of at most 0.0065.
Values may be sent and summed in bfloat16 or wider, within the bound.
A program may use at most 64 MiB of HBM per device.

v0:
```python
import jax
import jax.numpy as jnp
from jax import lax
from jax.sharding import PartitionSpec as P

D = 4096
HEADS = 64
KV_HEADS = 8
HD = 128
LEN = 4096
GROUP = 10


def normalize(stream, gain_vec):
    wide = stream.astype(jnp.float32)
    squares = lax.psum(jnp.sum(wide * wide, axis=1), ("section", "dp"))
    factor = lax.rsqrt(squares / D + 1e-05)
    return (wide * factor[:, None] * gain_vec[None, :]).astype(jnp.bfloat16)


def rotate(vector, cosine, sine_part):
    half_dim = vector.shape[-1] // 2
    first_half = vector[..., :half_dim]
    second = vector[..., half_dim:]
    return jnp.concatenate(
        [first_half * cosine - second * sine_part, second * cosine + first_half * sine_part],
        axis=-1,
    )


def project_rows(row_block, weight_cols):
    return jnp.dot(
        lax.all_gather(row_block, ("section", "dp"), axis=0, tiled=True),
        weight_cols,
        preferred_element_type=jnp.float32,
    )


def add_residual(base_rows, partial_sum):
    summed = lax.psum(partial_sum, "tensor")
    return (base_rows.astype(jnp.float32) + summed).astype(jnp.bfloat16)


def body(
    tokens,
    attn_gain,
    qkv_weight,
    qkv_order,
    cache_keys,
    cache_values,
    cache_len,
    out_weight,
    ffn_gain,
    gate_up,
    down_weight,
):
    seq_count = cache_len.shape[0]
    local_groups = cache_keys.shape[1]
    per_group = HEADS // KV_HEADS
    normed = normalize(tokens, attn_gain)
    row_block = normed
    joined_cols = lax.psum_scatter(
        jnp.dot(row_block, qkv_weight, preferred_element_type=jnp.float32),
        ("section", "dp"),
        scatter_dimension=0,
        tiled=True,
    )
    blocks = joined_cols.reshape(seq_count, local_groups, GROUP, HD)
    onehot = (qkv_order[:, None] == jnp.arange(GROUP, dtype=jnp.int32)[None, :]).astype(jnp.float32)
    logical = jnp.einsum("bgjd,ji->bgid", blocks, onehot, precision=lax.Precision.HIGHEST)
    half_dim = HD // 2
    inv_freq = 500000.0 ** (-(2.0 * jnp.arange(half_dim, dtype=jnp.float32)) / HD)
    angles = cache_len.astype(jnp.float32)[:, None] * inv_freq[None, :]
    cosine = jnp.cos(angles)
    sine_part = jnp.sin(angles)
    queries = rotate(
        logical[:, :, :per_group], cosine[:, None, None, :], sine_part[:, None, None, :]
    ).astype(jnp.bfloat16)
    new_key = rotate(logical[:, :, per_group], cosine[:, None, :], sine_part[:, None, :]).astype(
        jnp.bfloat16
    )
    new_value = logical[:, :, per_group + 1].astype(jnp.bfloat16)
    inv_scale = 1.0 / jnp.sqrt(jnp.float32(HD))
    scores = (
        jnp.einsum("bgpd,bgld->bgpl", queries, cache_keys, preferred_element_type=jnp.float32)
        * inv_scale
    )
    own_score = (
        jnp.einsum("bgpd,bgd->bgp", queries, new_key, preferred_element_type=jnp.float32)
        * inv_scale
    )
    valid_mask = jnp.arange(LEN, dtype=jnp.int32)[None, :] < cache_len[:, None]
    masked = jnp.where(valid_mask[:, None, None, :], scores, -jnp.inf)
    peak = jnp.maximum(jnp.max(masked, axis=-1), own_score)
    weights = jnp.exp(masked - peak[..., None])
    own_weight = jnp.exp(own_score - peak)
    denom_sum = jnp.sum(weights, axis=-1) + own_weight
    probabilities = (weights / denom_sum[..., None]).astype(jnp.bfloat16)
    own_prob = (own_weight / denom_sum).astype(jnp.bfloat16)
    mixed_heads = jnp.einsum(
        "bgpl,bgld->bgpd", probabilities, cache_values, preferred_element_type=jnp.float32
    )
    mixed_heads = (
        mixed_heads
        + own_prob.astype(jnp.float32)[..., None] * new_value.astype(jnp.float32)[:, :, None, :]
    )
    attended = mixed_heads.astype(jnp.bfloat16).reshape(seq_count, -1)
    hidden_state = add_residual(tokens, project_rows(attended, out_weight))
    ffn_normed = normalize(hidden_state, ffn_gain)
    row_block = ffn_normed
    gate_and_up = lax.psum_scatter(
        jnp.einsum("rd,kdf->rkf", row_block, gate_up, preferred_element_type=jnp.float32),
        ("section", "dp"),
        scatter_dimension=0,
        tiled=True,
    )
    activated = (jax.nn.silu(gate_and_up[:, 0]) * gate_and_up[:, 1]).astype(jnp.bfloat16)
    return add_residual(hidden_state, project_rows(activated, down_weight))


def solution(mesh):
    return jax.shard_map(
        body,
        mesh=mesh,
        in_specs=(
            P(None, ("section", "dp")),
            P(("section", "dp")),
            P(("section", "dp"), "tensor"),
            P(),
            P(("section", "dp"), "tensor", None, None),
            P(("section", "dp"), "tensor", None, None),
            P(("section", "dp")),
            P("tensor", ("section", "dp")),
            P(("section", "dp")),
            P(None, ("section", "dp"), "tensor"),
            P("tensor", ("section", "dp")),
        ),
        out_specs=P(None, ("section", "dp")),
        check_vma=False,
    )
```

profile of v0, /device:TPU:0, one launch (start us, length us, event | category | flops | bytes accessed | tf_op | source)
XLA Modules:
  0.0 227.4 jit_solution(6629242835967836412)
XLA Ops:
  6.5 1.0 fusion.7
  7.5 15.1 %psum.28 = f32[16]{0:T(128)S(1)} all-reduce(f32[16]{0:T(128)S(1)} %fusion.7), channel_id=1, replica_groups=mesh['section'=2,'tensor'=4,'dp'=4] {'section','dp'}, use_global_device_ids=true, to_apply=%region_1.0 | all-reduce | flops 16 | bytes 128 | tf_op jit(solution)/shard_map/psum | solution.py:16
  22.7 1.9 fusion.19
  24.6 0.7 convert_element_type.47
  25.3 0.7 iota_compare_fusion
  26.2 1.2 dynamic-slice
  28.1 48.3 %all-reduce.5.cloned.1.call-done = f32[16,2560]{1,0:T(8,128)} async-done(((f32[16,2560]{1,0:T(8,128)}), f32[16,2560]{1,0:T(8,128)}) %all-reduce.5.cloned.1.call-update) | async-done | bytes 163856
  76.4 0.9 constant_dynamic-slice_fusion
  77.3 0.9 convolution_bitcast_fusion
  78.5 0.2 fusion.29
  78.7 3.5 %fusion.36 = (f32[2,2,8]{2,1,0:T(2,128)S(1)}, f32[2,2,8,4096]{3,2,1,0:T(8,128)S(1)}) fusion(bf16[2,2,4096,128]{3,2,1,0:T(8,128)(2,1)} %param.15, bf16[2,2,8,64]{3,2,1,0:T(8,128)(2,1)S(1)} %get-tuple-element.8, bf16[2,2,8,64]{3,2,1,0:T(8,128)(2,1)S(1)} %get-tuple-element.7, pred[2,4096]{1,0:T(4,128)(4,1)S(1)} %iota_compare_fusion), kind=kOutput, calls=%fused_computation.64 | convolution fusion | flops 33964000 | bytes 4735104 | tf_op jit(solution)/shard_map/bgpd,bgld->bgpl/dot_general | solution.py:85
  82.3 0.2 fusion.2
  82.5 0.7 fusion.1
  83.3 10.0 %all-gather = bf16[8,2,2048]{2,1,0:T(2,128)(2,1)S(1)} all-gather(bf16[1,2,2048]{2,1,0:T(2,128)(2,1)S(1)} %reshape.129), channel_id=1, replica_groups=mesh['section'=2,'tensor'=4,'dp'=4] {'section','dp'}, dimensions={0}, use_global_device_ids=true | all-gather | bytes 73728 | tf_op jit(solution)/shard_map/all_gather | solution.py:33
  93.3 2.0 fusion.37
  95.3 19.0 %psum.29 = f32[16,512]{1,0:T(8,128)S(1)} all-reduce(f32[16,512]{1,0:T(8,128)S(1)} %fusion.37), channel_id=1, replica_groups=mesh['section'=2,'tensor'=4,'dp'=4] {'tensor'}, use_global_device_ids=true, to_apply=%region_5.6 | all-reduce | flops 8192 | bytes 65536 | tf_op jit(solution)/shard_map/psum | solution.py:40
  114.4 11.8 %psum.30 = f32[16]{0:T(128)S(1)} all-reduce(f32[16]{0:T(128)S(1)} %get-tuple-element.5), channel_id=1, replica_groups=mesh['section'=2,'tensor'=4,'dp'=4] {'section','dp'}, use_global_device_ids=true, to_apply=%region_7.8 | all-reduce | flops 16 | bytes 128 | tf_op jit(solution)/shard_map/psum | solution.py:16
  126.2 8.2 %fusion.17 = f32[16,2,7168]{2,0,1:T(8,128)} fusion(bf16[2,512,7168]{2,1,0:T(8,128)(2,1)} %param.20, bf16[16,512]{1,0:T(8,128)(2,1)S(1)} %get-tuple-element.6, f32[512]{0:T(512)S(1)} %copy-done.3, f32[16]{0:T(128)S(1)} %add_rsqrt_fusion), kind=kOutput, calls=%fused_computation.32 | convolution fusion | flops 234913792 | bytes 15616064 | tf_op jit(solution)/shard_map/rd,kdf->rkf/dot_general | solution.py:112
  134.4 52.6 %all-reduce.7.cloned.1.call-done = f32[16,2,7168]{2,0,1:T(8,128)} async-done(((f32[16,2,7168]{2,0,1:T(8,128)}), f32[16,2,7168]{2,0,1:T(8,128)}) %all-reduce.7.cloned.1.call-update) | async-done | bytes 917520
  187.1 1.1 fusion.15
  188.2 8.6 %all-gather.1 = bf16[8,2,7168]{2,1,0:T(2,128)(2,1)S(1)} all-gather(bf16[1,2,7168]{2,1,0:T(2,128)(2,1)S(1)} %fusion.15), channel_id=1, replica_groups=mesh['section'=2,'tensor'=4,'dp'=4] {'section','dp'}, dimensions={0}, use_global_device_ids=true | all-gather | bytes 258048 | tf_op jit(solution)/shard_map/all_gather | solution.py:33
  196.8 4.1 %fusion.38 = f32[16,512]{1,0:T(8,128)S(1)} fusion(bf16[16,7168]{1,0:T(8,128)(2,1)S(1)} %reshape.132, bf16[7168,512]{1,0:T(8,128)(2,1)} %param.21), kind=kOutput, calls=%fused_computation.66 | convolution fusion | flops 117440512 | bytes 7602176 | tf_op jit(solution)/shard_map/dot_general | solution.py:32
  201.0 19.0 %psum.31 = f32[16,512]{1,0:T(8,128)S(1)} all-reduce(f32[16,512]{1,0:T(8,128)S(1)} %fusion.38), channel_id=1, replica_groups=mesh['section'=2,'tensor'=4,'dp'=4] {'tensor'}, use_global_device_ids=true, to_apply=%region_9.10 | all-reduce | flops 8192 | bytes 65536 | tf_op jit(solution)/shard_map/psum | solution.py:40
  220.0 0.6 fusion.14
  (28 shorter events, 0.8 us)
Async XLA Ops:
  6.5 16.1 %copy-start = (bf16[512,2560]{1,0:T(8,128)(2,1)S(1)}, bf16[512,2560]{1,0:T(8,128)(2,1)}, u32[]{:S(2)}) copy-start(bf16[512,2560]{1,0:T(8,128)(2,1)} %param.13) | copy-start | bytes 7864324
  6.5 69.9 %all-reduce.5.cloned.1.call-start = ((), (), s32[]{:S(2)}) async-start(), calls=%async_computation | async-start | bytes 327680
  24.6 162.5 %all-reduce.7.cloned.1.call-start = ((), (), s32[]{:S(2)}) async-start(), calls=%async_computation.1 | async-start | bytes 1835008
  77.3 5.2 %copy-start.1 = (bf16[2,2,4096,128]{3,2,1,0:T(8,128)(2,1)S(1)}, bf16[2,2,4096,128]{3,2,1,0:T(8,128)(2,1)}, u32[]{:S(2)}) copy-start(bf16[2,2,4096,128]{3,2,1,0:T(8,128)(2,1)} %param.16) | copy-start | bytes 12582916
  82.2 32.0 %copy-start.2 = (bf16[16,512]{1,0:T(8,128)(2,1)S(1)}, bf16[16,512]{1,0:T(8,128)(2,1)}, u32[]{:S(2)}) copy-start(bf16[16,512]{1,0:T(8,128)(2,1)} %param.11) | copy-start | bytes 49156
  82.2 44.0 %copy-start.3 = (f32[512]{0:T(512)S(1)}, f32[512]{0:T(512)}, u32[]{:S(2)}) copy-start(f32[512]{0:T(512)} %param.19) | copy-start | bytes 6148
Sparse Core Ops, SparseCore 0:
  24.7 51.6 all-reduce.4
  134.6 52.4 all-reduce.6
where the time goes:
time: 228 us; the launch traced here: 227 us
  waiting for transfers between devices  101 us (44%)
  blocking collectives  83.5 us (37%)
  matrix products  21.5 us (9%)
  between operations  14.2 us (6%)
  other arithmetic  4.91 us (2%)
  local copies, waits for them, and re-layouts  2.31 us (1%)
    unnamed x4, waiting for transfers between devices  101 us
    psum x2, blocking collectives, add_residual(): summed = lax.psum(partial_sum, 'tensor')  38 us
    psum x2, blocking collectives, normalize(): squares = lax.psum(jnp.sum(wide * wide, axis=1), ('section', 'dp'))  27 us
    all_gather x2, blocking collectives, project_rows(): lax.all_gather(row_block, ('section', 'dp'), axis=0, tiled=True)  18.6 us
    dot_general x1, matrix products, body(): jnp.einsum('rd,kdf->rkf', row_block, gate_up, preferred_element_type=jnp....  8.21 us
    dot_general x2, matrix products, project_rows(): jnp.dot(lax.all_gather(row_block, ('section', 'dp'), axis=0, tiled=True),...  6.09 us
  transfers between devices with their start and end apart: 2, of which 2 were waited for; matrix products, arithmetic and copies ran while one was open for 1% of the time, Pallas kernels for 0%

commit v1 on v0

--- a/solution.py
+++ b/solution.py
@@ -37,7 +37,8 @@
 
 
 def add_residual(base_rows, partial_sum):
-    summed = lax.psum(partial_sum, "tensor")
+    parts = lax.all_gather(partial_sum, "tensor")
+    summed = jnp.sum(parts, axis=0)
     return (base_rows.astype(jnp.float32) + summed).astype(jnp.bfloat16)
 
 

time: 228 us -> 220 us (0.965)
  blocking collectives: 83.5 us -> 72.5 us
  waiting for transfers between devices: 101 us -> 104 us
    psum x2 -> x0, blocking collectives: 38 us -> none  [add_residual(): summed = lax.psum(partial_sum, 'tensor')]
    all_gather x0 -> x2, blocking collectives: none -> 27 us  [add_residual(): parts = lax.all_gather(partial_sum, 'tensor')]
    unnamed x4, waiting for transfers between devices: 101 us -> 104 us
where the time goes in v1:
time: 220 us; the launch traced here: 219 us
  waiting for transfers between devices  104 us (47%)
  blocking collectives  72.5 us (33%)
  matrix products  21.5 us (10%)
  between operations  14.2 us (6%)
  other arithmetic  4.93 us (2%)
  local copies, waits for them, and re-layouts  2.31 us (1%)
    unnamed x4, waiting for transfers between devices  104 us
    all_gather x2, blocking collectives, add_residual(): parts = lax.all_gather(partial_sum, 'tensor')  27 us
    psum x2, blocking collectives, normalize(): squares = lax.psum(jnp.sum(wide * wide, axis=1), ('section', 'dp'))  27 us
    all_gather x2, blocking collectives, project_rows(): lax.all_gather(row_block, ('section', 'dp'), axis=0, tiled=True)  18.6 us
    dot_general x1, matrix products, body(): jnp.einsum('rd,kdf->rkf', row_block, gate_up, preferred_element_type=jnp....  8.21 us
    dot_general x2, matrix products, project_rows(): jnp.dot(lax.all_gather(row_block, ('section', 'dp'), axis=0, tiled=True),...  6.09 us
  transfers between devices with their start and end apart: 2, of which 2 were waited for; matrix products, arithmetic and copies ran while one was open for 1% of the time, Pallas kernels for 0%

profile of v1, /device:TPU:0, one launch (start us, length us, event | category | flops | bytes accessed | tf_op | source)
XLA Modules:
  0.0 219.2 jit_solution(9912678793520250653)
XLA Ops:
  6.5 1.0 fusion.7
  7.5 15.1 %psum.14 = f32[16]{0:T(128)S(1)} all-reduce(f32[16]{0:T(128)S(1)} %fusion.7), channel_id=1, replica_groups=mesh['section'=2,'tensor'=4,'dp'=4] {'section','dp'}, use_global_device_ids=true, to_apply=%region_1.0 | all-reduce | flops 16 | bytes 128 | tf_op jit(solution)/shard_map/psum | solution.py:16
  22.7 1.9 fusion.19
  24.6 0.7 convert_element_type.47
  25.3 0.7 iota_compare_fusion
  26.2 1.2 dynamic-slice
  28.1 48.3 %all-reduce.5.cloned.1.call-done = f32[16,2560]{1,0:T(8,128)} async-done(((f32[16,2560]{1,0:T(8,128)}), f32[16,2560]{1,0:T(8,128)}) %all-reduce.5.cloned.1.call-update) | async-done | bytes 163856
  76.4 0.9 constant_dynamic-slice_fusion
  77.3 0.9 convolution_bitcast_fusion
  78.5 0.2 fusion.29
  78.7 3.5 %fusion.36 = (f32[2,2,8]{2,1,0:T(2,128)S(1)}, f32[2,2,8,4096]{3,2,1,0:T(8,128)S(1)}) fusion(bf16[2,2,4096,128]{3,2,1,0:T(8,128)(2,1)} %param.15, bf16[2,2,8,64]{3,2,1,0:T(8,128)(2,1)S(1)} %get-tuple-element.8, bf16[2,2,8,64]{3,2,1,0:T(8,128)(2,1)S(1)} %get-tuple-element.7, pred[2,4096]{1,0:T(4,128)(4,1)S(1)} %iota_compare_fusion), kind=kOutput, calls=%fused_computation.64 | convolution fusion | flops 33964000 | bytes 4735104 | tf_op jit(solution)/shard_map/bgpd,bgld->bgpl/dot_general | solution.py:86
  82.3 0.2 fusion.2
  82.5 0.7 fusion.1
  83.3 10.0 %all-gather.2 = bf16[8,2,2048]{2,1,0:T(2,128)(2,1)S(1)} all-gather(bf16[1,2,2048]{2,1,0:T(2,128)(2,1)S(1)} %reshape.131), channel_id=1, replica_groups=mesh['section'=2,'tensor'=4,'dp'=4] {'section','dp'}, dimensions={0}, use_global_device_ids=true | all-gather | bytes 73728 | tf_op jit(solution)/shard_map/all_gather | solution.py:33
  93.3 2.0 fusion.37
  95.3 13.5 %all-gather = f32[64,512]{1,0:T(8,128)S(1)} all-gather(f32[16,512]{1,0:T(8,128)S(1)} %fusion.37), channel_id=2, replica_groups=mesh['section'=2,'tensor'=4,'dp'=4] {'tensor'}, dimensions={0}, use_global_device_ids=true | all-gather | bytes 163840 | tf_op jit(solution)/shard_map/all_gather | solution.py:40
  108.9 11.8 %psum.15 = f32[16]{0:T(128)S(1)} all-reduce(f32[16]{0:T(128)S(1)} %get-tuple-element.5), channel_id=1, replica_groups=mesh['section'=2,'tensor'=4,'dp'=4] {'section','dp'}, use_global_device_ids=true, to_apply=%region_7.8 | all-reduce | flops 16 | bytes 128 | tf_op jit(solution)/shard_map/psum | solution.py:16
  120.7 8.2 %fusion.17 = f32[16,2,7168]{2,0,1:T(8,128)} fusion(bf16[2,512,7168]{2,1,0:T(8,128)(2,1)} %param.20, bf16[16,512]{1,0:T(8,128)(2,1)S(1)} %get-tuple-element.6, f32[512]{0:T(512)S(1)} %copy-done.3, f32[16]{0:T(128)S(1)} %add_rsqrt_fusion), kind=kOutput, calls=%fused_computation.32 | convolution fusion | flops 234913792 | bytes 15616064 | tf_op jit(solution)/shard_map/rd,kdf->rkf/dot_general | solution.py:113
  129.0 55.4 %all-reduce.7.cloned.1.call-done = f32[16,2,7168]{2,0,1:T(8,128)} async-done(((f32[16,2,7168]{2,0,1:T(8,128)}), f32[16,2,7168]{2,0,1:T(8,128)}) %all-reduce.7.cloned.1.call-update) | async-done | bytes 917520
  184.4 1.1 fusion.15
  185.5 8.6 %all-gather.3 = bf16[8,2,7168]{2,1,0:T(2,128)(2,1)S(1)} all-gather(bf16[1,2,7168]{2,1,0:T(2,128)(2,1)S(1)} %fusion.15), channel_id=1, replica_groups=mesh['section'=2,'tensor'=4,'dp'=4] {'section','dp'}, dimensions={0}, use_global_device_ids=true | all-gather | bytes 258048 | tf_op jit(solution)/shard_map/all_gather | solution.py:33
  194.1 4.1 %fusion.38 = f32[16,512]{1,0:T(8,128)S(1)} fusion(bf16[16,7168]{1,0:T(8,128)(2,1)S(1)} %reshape.134, bf16[7168,512]{1,0:T(8,128)(2,1)} %param.21), kind=kOutput, calls=%fused_computation.66 | convolution fusion | flops 117440512 | bytes 7602176 | tf_op jit(solution)/shard_map/dot_general | solution.py:32
  198.3 13.5 %all-gather.1 = f32[64,512]{1,0:T(8,128)S(1)} all-gather(f32[16,512]{1,0:T(8,128)S(1)} %fusion.38), channel_id=3, replica_groups=mesh['section'=2,'tensor'=4,'dp'=4] {'tensor'}, dimensions={0}, use_global_device_ids=true | all-gather | bytes 163840 | tf_op jit(solution)/shard_map/all_gather | solution.py:40
  211.8 0.6 fusion.14
  (30 shorter events, 0.8 us)
Async XLA Ops:
  6.5 16.1 %copy-start = (bf16[512,2560]{1,0:T(8,128)(2,1)S(1)}, bf16[512,2560]{1,0:T(8,128)(2,1)}, u32[]{:S(2)}) copy-start(bf16[512,2560]{1,0:T(8,128)(2,1)} %param.13) | copy-start | bytes 7864324
  6.5 69.9 %all-reduce.5.cloned.1.call-start = ((), (), s32[]{:S(2)}) async-start(), calls=%async_computation | async-start | bytes 327680
  24.6 159.8 %all-reduce.7.cloned.1.call-start = ((), (), s32[]{:S(2)}) async-start(), calls=%async_computation.1 | async-start | bytes 1835008
  77.3 5.2 %copy-start.1 = (bf16[2,2,4096,128]{3,2,1,0:T(8,128)(2,1)S(1)}, bf16[2,2,4096,128]{3,2,1,0:T(8,128)(2,1)}, u32[]{:S(2)}) copy-start(bf16[2,2,4096,128]{3,2,1,0:T(8,128)(2,1)} %param.16) | copy-start | bytes 12582916
  82.2 26.5 %copy-start.2 = (bf16[16,512]{1,0:T(8,128)(2,1)S(1)}, bf16[16,512]{1,0:T(8,128)(2,1)}, u32[]{:S(2)}) copy-start(bf16[16,512]{1,0:T(8,128)(2,1)} %param.11) | copy-start | bytes 49156
  82.2 38.5 %copy-start.3 = (f32[512]{0:T(512)S(1)}, f32[512]{0:T(512)}, u32[]{:S(2)}) copy-start(f32[512]{0:T(512)} %param.19) | copy-start | bytes 6148
Sparse Core Ops, SparseCore 0:
  24.7 51.6 all-reduce.4
  129.1 55.2 all-reduce.6
